TPU v7x, 8 devices: a whole 2x2x1 slice. The times are simulated.
8 devices in a mesh: dp: 1 (over z), vblk: 2 (over y), vocab: 4 (over x, core).
Axes of the slice: x: 2, y: 2, z: 1, core: 2. Of those that a mesh axis runs over, the one named last changes fastest.
Arguments:
- hidden: bfloat16 [16, 3072], P('dp')
- w_head: bfloat16 [3072, 256000], P(None, ('vblk', 'vocab'))
- inv_temp: float32 [16], P('dp')
- target: int32 [16], P('dp')
Outputs:
- output 1: float32 [16, 256000], P('dp', ('vblk', 'vocab'))
- output 2: float32 [16], P('dp')
All inputs are finite; a program needn't handle non-finite values.
Results may differ from a plain program's by a relative error of at most 0.001.
Values are sent between devices in bfloat16 or wider.
A program may use at most 1 GiB of HBM per device.

v0:
```python
import jax
import jax.numpy as jnp
from jax import lax
from jax.sharding import PartitionSpec as P


def solution(mesh):
    vocab_axes = ("vblk", "vocab")
    vocab_size = mesh.shape["vocab"]
    shard_count = mesh.shape["vblk"] * vocab_size

    def local_step(hidden, w_head, inv_temp, target):
        shard_width = w_head.shape[1]
        shard_idx = lax.axis_index("vblk") * vocab_size + lax.axis_index("vocab")
        logits = jnp.dot(hidden, w_head, preferred_element_type=jnp.float32) * inv_temp[:, None]
        local_max = jnp.max(logits, axis=1)
        exp_val = jnp.exp(logits - local_max[:, None])
        local_sum = jnp.sum(exp_val, axis=1)
        stat_pairs = lax.all_gather(jnp.stack([local_max, local_sum]), vocab_axes)
        glob_max = jnp.max(stat_pairs[:, 0], axis=0)
        glob_sum = jnp.sum(stat_pairs[:, 1] * jnp.exp(stat_pairs[:, 0] - glob_max[None, :]), axis=0)
        rescale = jnp.exp(local_max - glob_max) / glob_sum
        cdf_loc = jnp.cumsum(exp_val * rescale[:, None], axis=1)
        totals = lax.all_gather(cdf_loc[:, -1], vocab_axes)
        lower_shard = jnp.arange(shard_count) < shard_idx
        offset = jnp.sum(jnp.where(lower_shard[:, None], totals, 0.0), axis=0)
        cdf_table = cdf_loc + offset[:, None]
        col_ids = shard_idx * shard_width + jnp.arange(shard_width)
        is_target = col_ids[None, :] == target[:, None]
        picked = lax.psum(jnp.sum(jnp.where(is_target, cdf_table, 0.0), axis=1), vocab_axes)
        return cdf_table, picked

    return jax.shard_map(local_step, mesh=mesh, in_specs=(P("dp", None), P(None, vocab_axes), P("dp"), P("dp")), out_specs=(P("dp", vocab_axes), P("dp")), check_vma=False)
```

profile of v0, /device:TPU:0, one launch (start us, length us, event | category | flops | bytes accessed | tf_op | source)
XLA Modules:
  0.0 143.5 jit_solution(8727925796703534325)
XLA Ops:
  0.6 0.0 copy-start
  0.6 0.9 copy-done
  1.5 61.5 %fusion.3 = (f32[16]{0:T(128)S(1)}, f32[16,32000]{1,0:T(8,128)S(1)}) fusion(f32[16]{0:T(128)} %param.6, bf16[16,3072]{1,0:T(8,128)(2,1)S(1)} %copy-done, bf16[3072,32000]{1,0:T(8,128)(2,1)} %param.5), kind=kOutput, calls=%fused_computation.23 | convolution fusion | flops 3146752000 | bytes 198754432 | tf_op jit(solution)/shard_map/dot_general | solution.py:15
  63.0 0.6 fusion.1
  63.6 13.5 %all-gather.2 = f32[8,2,16]{2,1,0:T(2,128)S(1)} all-gather(f32[1,2,16]{2,1,0:T(2,128)S(1)} %maximum_bitcast_fusion), channel_id=2, replica_groups=mesh['dp'=1,'vblk'=2,'vocab'=4] {'vblk','vocab'}, dimensions={0}, use_global_device_ids=true | all-gather | bytes 1152 | tf_op jit(solution)/shard_map/all_gather | solution.py:19
  77.2 1.6 %fusion = f32[16,32000]{1,0:T(8,128)} fusion(f32[16,32000]{1,0:T(8,128)S(1)} %get-tuple-element.5, f32[16]{0:T(128)S(1)} %exponential_divide_fusion, f32[16]{0:T(128)S(1)} %get-tuple-element.4), kind=kLoop, calls=%fused_computation.4 | loop fusion | flops 1024000 | bytes 4096128 | tf_op jit(solution)/shard_map/mul | solution.py:23
  78.9 1.9 %reshape.61 = f32[16,250,128]{2,1,0:T(8,128)S(1)} reshape(f32[16,32000]{1,0:T(8,128)} %fusion) | data formatting | bytes 4096000 | tf_op jit(solution)/shard_map/reshape
  80.8 2.1 %copy.14 = f32[16,250,128]{1,0,2:T(8,128)} copy(f32[16,250,128]{2,1,0:T(8,128)S(1)} %reshape.61) | data formatting | bytes 4096000 | tf_op jit(solution)/shard_map/reshape
  82.8 1.8 %fusion.4 = f32[16,250,128]{1,0,2:T(8,128)S(1)} fusion(f32[16,250,128]{1,0,2:T(8,128)} %copy.14), kind=kOutput, calls=%fused_computation.24 | output fusion | flops 65024000 | bytes 4096000 | tf_op jit(solution)/shard_map/reduce-window
  84.6 0.6 reduce-window.14
  85.2 0.2 slice_reduce_fusion
  85.4 0.1 copy_bitcast_fusion.1
  85.5 0.1 pad_slice_fusion
  85.6 1.6 %broadcast_add_fusion = f32[16,250,128]{1,0,2:T(8,128)} fusion(f32[16,250,128]{1,0,2:T(8,128)S(1)} %fusion.4, f32[16,250]{1,0:T(8,128)S(1)} %pad_slice_fusion), kind=kLoop, calls=%fused_computation.6 | loop fusion | flops 512000 | bytes 4112000 | tf_op jit(solution)/shard_map/reduce_window_sum
  87.1 2.9 %copy.17 = f32[16,250,128]{2,1,0:T(8,128)} copy(f32[16,250,128]{1,0,2:T(8,128)} %broadcast_add_fusion) | data formatting | bytes 4096000 | tf_op jit(solution)/shard_map/reduce_window_sum
  90.1 0.0 copy-start.1
  90.1 2.8 %copy.28 = f32[2,8,250,128]{3,1,2,0:T(8,128)S(1)} copy(f32[2,8,250,128]{3,2,1,0:T(8,128)} %bitcast.32) | data formatting | bytes 4096000
  92.9 0.2 slice_reduce_fusion.1
  93.1 0.2 dynamic-update-slice
  93.3 22.2 %all-reduce.2 = f32[128]{0:T(128)S(1)} all-reduce(f32[128]{0:T(128)S(1)} %dynamic-update-slice), channel_id=3, replica_groups=mesh['dp'=1,'vblk'=2,'vocab'=4] {'vblk','vocab'}, use_global_device_ids=true, to_apply=%add.2 | all-reduce | flops 128 | bytes 1024
  115.5 0.1 reshape.66
  115.6 0.1 select_reduce_fusion.1
  115.7 0.0 copy-done.1
  115.7 0.6 select_reduce_fusion
  116.4 23.0 %psum.7 = f32[16]{0:T(128)} all-reduce(f32[16]{0:T(128)S(1)} %select_reduce_fusion), channel_id=1, replica_groups=mesh['dp'=1,'vblk'=2,'vocab'=4] {'vblk','vocab'}, use_global_device_ids=true, to_apply=%region_9.10 | all-reduce | flops 16 | bytes 128 | tf_op jit(solution)/shard_map/psum | solution.py:30
  139.4 4.1 %broadcast_add_fusion.1 = f32[16,32000]{1,0:T(8,128)} fusion(f32[16]{0:T(128)S(1)} %select_reduce_fusion.1, f32[2,8,250,128]{3,2,1,0:T(8,128)} %bitcast.33), kind=kLoop, calls=%fused_computation.7 | loop fusion | flops 512000 | bytes 4096064 | tf_op jit(solution)/shard_map/add | solution.py:27
  (12 shorter events, 0.2 us)
Async XLA Ops:
  0.6 0.9 copy-start
  90.1 25.6 %copy-start.1 = (s32[16]{0:T(128)S(1)}, s32[16]{0:T(128)}, u32[]{:S(2)}) copy-start(s32[16]{0:T(128)} %param.7) | copy-start | bytes 196
where the time goes:
time: 144 us; the launch traced here: 143 us
  matrix products  61.5 us (43%)
  blocking collectives  58.8 us (41%)
  local copies, waits for them, and re-layouts  11.3 us (8%)
  other arithmetic  11.2 us (8%)
    dot_general x1, matrix products, local_step(): jnp.dot(hidden, w_head, preferred_element_type=jnp.float32)  61.5 us
    psum x1, blocking collectives, local_step(): lax.psum(jnp.sum(jnp.where(is_target, cdf_table, 0.0), axis=1), vocab_axes)  23 us
    unnamed x1, blocking collectives  22.2 us
    all_gather x1, blocking collectives, local_step(): stat_pairs = lax.all_gather(jnp.stack([local_max, local_sum]), vocab_axes)  13.5 us
    add x1, other arithmetic, local_step(): cdf_table = cdf_loc + offset[:, None]  4.08 us
    another operation x5, other arithmetic  4.06 us
    reshape x2, local copies, waits for them, and re-layouts  3.93 us
    unnamed x7, local copies, waits for them, and re-layouts  3.93 us

commit v1 on v0

v1 whole, which is shorter than its diff:
```python
import functools

import jax
import jax.numpy as jnp
from jax import lax
from jax.experimental import pallas as pl
from jax.experimental.pallas import tpu as pltpu
from jax.sharding import PartitionSpec as P

MESH = pl.DeviceIdType.MESH
LANES = 128
GROUP = 256
TILE = 1024
TAPER = (512, 512, 256)
RING = 6


def stream_kernel(
    vblk_size, vocab_size, tau_hbm, tgt_hbm, h_hbm, w_hbm, c_ref, fin_ref,
    h_buf, w_buf, tri, run_max, pack, comm, tau_sm, tgt_sm, in_sem, w_sem, send_sem, recv_sem,
):
    n_dev = vblk_size * vocab_size
    rows = h_buf.shape[0]
    width = w_hbm.shape[1]
    n_full = (width - sum(TAPER)) // TILE
    me = lax.axis_index("vblk") * vocab_size + lax.axis_index("vocab")

    def peer_id(d):
        peer = lax.rem(me + d, n_dev)
        return {"vblk": lax.div(peer, vocab_size), "vocab": lax.rem(peer, vocab_size)}

    def w_copy(col, size, slot):
        return pltpu.make_async_copy(
            w_hbm.at[:, pl.ds(col, size)], w_buf.at[slot, :, pl.ds(0, size)], w_sem.at[slot]
        )

    small = [
        pltpu.make_async_copy(h_hbm, h_buf, in_sem.at[0]),
        pltpu.make_async_copy(tau_hbm, tau_sm, in_sem.at[1]),
        pltpu.make_async_copy(tgt_hbm, tgt_sm, in_sem.at[2]),
    ]
    for copy in small:
        copy.start()
    for t in range(RING):
        w_copy(t * TILE, TILE, t).start()

    barrier = pltpu.get_barrier_semaphore()
    for d in range(1, n_dev):
        pl.semaphore_signal(barrier, inc=1, device_id=peer_id(d), device_id_type=MESH)

    below = lax.broadcasted_iota(jnp.int32, tri.shape, 0)
    across = lax.broadcasted_iota(jnp.int32, tri.shape, 1)
    tri[...] = jnp.where((across >= GROUP) | (below <= across), 1.0, 0.0).astype(tri.dtype)

    for copy in small:
        copy.wait()
    row_id = lax.broadcasted_iota(jnp.int32, (rows, LANES), 0)
    lane_id = lax.broadcasted_iota(jnp.int32, (rows, LANES), 1)
    tau = jnp.zeros((rows, LANES), jnp.float32)
    tgt = jnp.zeros((rows, LANES), jnp.int32)
    for b in range(rows):
        tau = jnp.where(row_id == b, tau_sm[b], tau)
        tgt = jnp.where(row_id == b, tgt_sm[b], tgt)
    tgt_local = tgt - me * width

    def tile_step(index, col, size, slot, state):
        top, base, pick = state
        blocks, groups = size // LANES, size // GROUP
        z = jnp.dot(h_buf[...], w_buf[slot, :, pl.ds(0, size)], preferred_element_type=jnp.float32)
        z = [z[:, j * LANES:(j + 1) * LANES] * tau for j in range(blocks)]
        peak = functools.reduce(jnp.maximum, z)
        new_top = jnp.maximum(top, jnp.max(peak, axis=1, keepdims=True))
        alpha = jnp.exp(top - new_top)
        e = [jnp.exp(zj - new_top) for zj in z]
        e = jnp.concatenate([jnp.concatenate(e[2 * g:2 * g + 2], axis=1) for g in range(groups)], axis=0)
        hi = e.astype(jnp.bfloat16)
        rest = e - hi.astype(jnp.float32)
        mid = rest.astype(jnp.bfloat16)
        low = (rest - mid.astype(jnp.float32)).astype(jnp.bfloat16)
        sums = jnp.dot(jnp.concatenate([hi, mid, low], axis=0), tri[...], preferred_element_type=jnp.float32)
        n = rows * groups
        sums = sums[:n] + (sums[n:2 * n] + sums[2 * n:])
        base = base * alpha
        pick = pick * alpha
        hit = tgt_local - col
        for g in range(groups):
            part = sums[g * rows:(g + 1) * rows]
            for half in range(2):
                j = 2 * g + half
                value = part[:, half * LANES:(half + 1) * LANES] + base
                c_ref[:, pl.ds(col + j * LANES, LANES)] = value
                pick = pick + jnp.where(lane_id == hit - j * LANES, value, 0.0)
            base = base + part[:, GROUP:]
        run_max[index] = new_top
        return new_top, base, pick

    taper_cols = [n_full * TILE + sum(TAPER[:i]) for i in range(len(TAPER))]

    def full_step(t, state):
        slot = lax.rem(t, RING)
        w_copy(0, TILE, slot).wait()
        col = pl.multiple_of(t * TILE, TILE)
        state = tile_step(t, col, TILE, slot, state)

        @pl.when(t + RING < n_full)
        def _():
            w_copy(pl.multiple_of((t + RING) * TILE, TILE), TILE, slot).start()

        for i, (tcol, size) in enumerate(zip(taper_cols, TAPER)):
            @pl.when(t + RING == n_full + i)
            def _():
                w_copy(tcol, size, (n_full + i) % RING).start()

        return state

    zero = jnp.zeros((rows, LANES), jnp.float32)
    state = lax.fori_loop(0, n_full, full_step, (jnp.full((rows, LANES), -jnp.inf, jnp.float32), zero, zero))
    for i, (tcol, size) in enumerate(zip(taper_cols, TAPER)):
        slot = (n_full + i) % RING
        w_copy(tcol, size, slot).wait()
        state = tile_step(n_full + i, tcol, size, slot, state)
    top, total, pick = state

    diag = row_id == lane_id
    to_lanes = lambda x: jnp.sum(jnp.where(diag, x, 0.0), axis=0, keepdims=True)
    top_l = to_lanes(top)
    total_l = to_lanes(total)
    pick_l = to_lanes(jnp.broadcast_to(jnp.sum(pick, axis=1, keepdims=True), pick.shape))
    tgt_l = jnp.sum(jnp.where(diag, tgt, 0), axis=0, keepdims=True)
    sub = lax.broadcasted_iota(jnp.int32, (8, LANES), 0)
    packet = jnp.where(sub == 0, top_l, jnp.where(sub == 1, total_l, jnp.where(sub == 2, pick_l, 0.0)))
    pack[...] = packet
    comm[me] = packet

    pl.semaphore_wait(barrier, n_dev - 1)
    copies = [
        pltpu.make_async_remote_copy(
            src_ref=pack, dst_ref=comm.at[me], send_sem=send_sem.at[d - 1], recv_sem=recv_sem.at[d - 1],
            device_id=peer_id(d), device_id_type=MESH,
        )
        for d in range(1, n_dev)
    ]
    for copy in copies:
        copy.start()

    def rescale(index, col, size):
        factor = jnp.exp(run_max[index] - top)
        for j in range(size // LANES):
            cols = pl.ds(col + j * LANES, LANES)
            c_ref[:, cols] = c_ref[:, cols] * factor

    def rescale_full(t, carry):
        rescale(t, pl.multiple_of(t * TILE, TILE), TILE)
        return carry

    lax.fori_loop(0, n_full, rescale_full, 0)
    for i, (tcol, size) in enumerate(zip(taper_cols, TAPER)):
        rescale(n_full + i, tcol, size)

    for copy in copies:
        copy.wait()
    tops, sums, picks = comm[:, 0, :], comm[:, 1, :], comm[:, 2, :]
    top_all = jnp.max(tops, axis=0, keepdims=True)
    scale = jnp.exp(tops - top_all)
    mass = sums * scale
    dev = lax.broadcasted_iota(jnp.int32, (n_dev, LANES), 0)
    all_mass = jnp.sum(mass, axis=0, keepdims=True)
    lower = jnp.sum(jnp.where(dev < me, mass, 0.0), axis=0, keepdims=True)
    lower_tgt = jnp.sum(jnp.where((dev + 1) * width <= tgt_l, mass, 0.0), axis=0, keepdims=True)
    picked = jnp.sum(picks * scale, axis=0, keepdims=True) + lower_tgt
    mult = jnp.exp(top_l - top_all) / all_mass
    fin_ref[...] = jnp.where(
        sub == 0, mult, jnp.where(sub == 1, lower / all_mass, jnp.where(sub == 2, picked / all_mass, 0.0))
    )


def solution(mesh):
    vblk_size, vocab_size = mesh.shape["vblk"], mesh.shape["vocab"]
    n_dev = vblk_size * vocab_size

    def local_step(hidden, w_head, inv_temp, target):
        rows, depth = hidden.shape
        width = w_head.shape[1]
        n_tiles = (width - sum(TAPER)) // TILE + len(TAPER)
        hbm = pl.BlockSpec(memory_space=pltpu.HBM)
        vmem = pl.BlockSpec(memory_space=pltpu.VMEM)
        mass, fin = pl.pallas_call(
            functools.partial(stream_kernel, vblk_size, vocab_size),
            out_shape=(
                jax.ShapeDtypeStruct((rows, width), jnp.float32),
                jax.ShapeDtypeStruct((8, LANES), jnp.float32),
            ),
            in_specs=[hbm] * 4,
            out_specs=(vmem, vmem),
            scratch_shapes=[
                pltpu.VMEM((rows, depth), jnp.bfloat16),
                pltpu.VMEM((RING, depth, TILE), jnp.bfloat16),
                pltpu.VMEM((GROUP, GROUP + LANES), jnp.bfloat16),
                pltpu.VMEM((n_tiles, rows, LANES), jnp.float32),
                pltpu.VMEM((8, LANES), jnp.float32),
                pltpu.VMEM((n_dev, 8, LANES), jnp.float32),
                pltpu.SMEM((rows,), jnp.float32),
                pltpu.SMEM((rows,), jnp.int32),
                pltpu.SemaphoreType.DMA((3,)),
                pltpu.SemaphoreType.DMA((RING,)),
                pltpu.SemaphoreType.DMA((n_dev - 1,)),
                pltpu.SemaphoreType.DMA((n_dev - 1,)),
            ],
            compiler_params=pltpu.CompilerParams(
                collective_id=0, has_side_effects=True, vmem_limit_bytes=48 * 1024 * 1024
            ),
        )(*[pltpu.with_memory_space_constraint(x, pltpu.HBM) for x in (inv_temp, target, hidden, w_head)])
        cdf = mass * fin[0, :rows, None] + fin[1, :rows, None]
        return cdf, fin[2, :rows]

    vocab_axes = ("vblk", "vocab")
    return jax.shard_map(
        local_step,
        mesh=mesh,
        in_specs=(P("dp", None), P(None, vocab_axes), P("dp"), P("dp")),
        out_specs=(P("dp", vocab_axes), P("dp")),
        check_vma=False,
    )
```

time: 144 us -> 68.2 us (0.47)
  Pallas kernels: 0 us -> 65.4 us
  matrix products: 61.5 us -> 0 us
  blocking collectives: 58.8 us -> 0 us
  local copies, waits for them, and re-layouts: 11.3 us -> 0.51 us
  other arithmetic: 11.2 us -> 1.53 us
    pallas_call x0 -> x1, Pallas kernels: none -> 65.4 us  [local_step(): pl.pallas_call(functools.partial(stream_kernel, vblk_size, vocab_size), o...]
    dot_general x1 -> x0, matrix products: 61.5 us -> none  [local_step(): jnp.dot(hidden, w_head, preferred_element_type=jnp.float32)]
    psum x1 -> x0, blocking collectives: 23 us -> none  [local_step(): lax.psum(jnp.sum(jnp.where(is_target, cdf_table, 0.0), axis=1), vocab_axes)]
    unnamed x1 -> x0, blocking collectives: 22.2 us -> none
    all_gather x1 -> x0, blocking collectives: 13.5 us -> none  [local_step(): stat_pairs = lax.all_gather(jnp.stack([local_max, local_sum]), vocab_axes)]
    another operation x5 -> x0, other arithmetic: 4.06 us -> none
    reshape x2 -> x0, local copies, waits for them, and re-layouts: 3.93 us -> none
    unnamed x7 -> x0, local copies, waits for them, and re-layouts: 3.93 us -> none
where the time goes in v1:
time: 68.2 us; the launch traced here: 68.1 us
  Pallas kernels  65.4 us (96%)
  other arithmetic  1.53 us (2%)
    pallas_call x1, Pallas kernels, local_step(): pl.pallas_call(functools.partial(stream_kernel, vblk_size, vocab_size), o...  65.4 us
    add x1, other arithmetic, local_step(): cdf = mass * fin[0, :rows, None] + fin[1, :rows, None]  1.53 us

profile of v1, /device:TPU:0, one launch (start us, length us, event | category | flops | bytes accessed | tf_op | source)
XLA Modules:
  0.0 68.1 jit_solution(17564102412605835883)
XLA Ops:
  0.6 65.4 %shard_map.59 = (f32[16,32000]{1,0:T(8,128)S(1)}, f32[8,128]{1,0:T(8,128)S(1)}) custom-call(f32[16]{0:T(128)} %tau_hbm.1, s32[16]{0:T(128)} %tgt_hbm.1, bf16[16,3072]{1,0:T(8,128)(2,1)} %h_hbm.1, bf16[3072,32000]{1,0:T(8,128)(2,1)} %w_hbm.1), custom_call_target="tpu_custom_call" | custom-call | tf_op jit(solution)/shard_map/pallas_call | solution.py:187
  66.0 0.5 slice_bitcast_fusion
  66.5 1.5 %multiply_add_fusion = f32[16,32000]{1,0:T(8,128)} fusion(f32[16,32000]{1,0:T(8,128)S(1)} %get-tuple-element.4, f32[16]{0:T(128)S(1)} %get-tuple-element.7, f32[16]{0:T(128)S(1)} %get-tuple-element.8), kind=kLoop, calls=%fused_computation | loop fusion | flops 1024000 | bytes 4096128 | tf_op jit(solution)/shard_map/add | solution.py:213

commit v2 on v1

v2 whole, which is shorter than its diff:
```python
import functools

import jax
import jax.numpy as jnp
from jax import lax
from jax.experimental import pallas as pl
from jax.experimental.pallas import tpu as pltpu
from jax.sharding import PartitionSpec as P

MESH = pl.DeviceIdType.MESH
LANES = 128
GROUP = 256
TILE = 1280
CHUNKS = 6
RING = 3
PUSH = 512
PUSHES = 10
SLOTS = 4
OUT_CHUNKS = 5


def split_sums(e, tri):
    hi = e.astype(jnp.bfloat16)
    rest = e - hi.astype(jnp.float32)
    mid = rest.astype(jnp.bfloat16)
    low = (rest - mid.astype(jnp.float32)).astype(jnp.bfloat16)
    sums = jnp.dot(jnp.concatenate([hi, mid, low], axis=0), tri[...], preferred_element_type=jnp.float32)
    n = e.shape[0]
    return sums[:n] + (sums[n:2 * n] + sums[2 * n:])


def stream_kernel(
    vblk_size, vocab_size, tau_hbm, tgt_hbm, h_hbm, w_hbm, c_ref, fin_ref,
    h_buf, w_buf, push_buf, z_out, z_in, tri, near_max, far_max, far, pack, comm, tau_sm, tgt_sm,
    in_sem, w_sem, last_sem, push_send, push_recv, z_send, z_recv, send_sem, recv_sem,
):
    n_dev = vblk_size * vocab_size
    rows, depth = h_buf.shape
    width = w_hbm.shape[1]
    pushed = PUSH * PUSHES
    n_full = (width - pushed) // TILE - 1
    part = depth // CHUNKS
    vblk, vocab = lax.axis_index("vblk"), lax.axis_index("vocab")
    me = vblk * vocab_size + vocab
    chip, core = lax.div(vocab, 2), lax.rem(vocab, 2)
    sibling = {"vblk": vblk, "vocab": chip * 2 + (1 - core)}

    def peer_id(d):
        peer = lax.rem(me + d, n_dev)
        return {"vblk": lax.div(peer, vocab_size), "vocab": lax.rem(peer, vocab_size)}

    def near_col(t):
        return pl.multiple_of(pushed + t * TILE, LANES)

    def far_col(p):
        return pl.multiple_of(p * PUSH, LANES)

    def w_copy(t, slot):
        return pltpu.make_async_copy(w_hbm.at[:, pl.ds(near_col(t), TILE)], w_buf.at[slot], w_sem.at[slot])

    def last_copy(k):
        return pltpu.make_async_copy(
            w_hbm.at[pl.ds(k * part, part), pl.ds(near_col(n_full), TILE)],
            w_buf.at[n_full % RING, pl.ds(k * part, part)],
            last_sem.at[k],
        )

    def push_copy(p):
        return pltpu.make_async_remote_copy(
            src_ref=w_hbm.at[:, pl.ds(far_col(p), PUSH)], dst_ref=push_buf.at[p % SLOTS],
            send_sem=push_send.at[p], recv_sem=push_recv.at[p], device_id=sibling, device_id_type=MESH,
        )

    def z_copy(p):
        return pltpu.make_async_remote_copy(
            src_ref=z_out.at[p], dst_ref=z_in.at[p],
            send_sem=z_send.at[p], recv_sem=z_recv.at[p], device_id=sibling, device_id_type=MESH,
        )

    barrier = pltpu.get_barrier_semaphore()
    for d in range(1, n_dev):
        pl.semaphore_signal(barrier, inc=1, device_id=peer_id(d), device_id_type=MESH)

    small = [
        pltpu.make_async_copy(h_hbm, h_buf, in_sem.at[0]),
        pltpu.make_async_copy(tau_hbm, tau_sm, in_sem.at[1]),
        pltpu.make_async_copy(tgt_hbm, tgt_sm, in_sem.at[2]),
    ]
    for copy in small:
        copy.start()
    for t in range(RING):
        w_copy(t, t).start()

    pl.semaphore_wait(barrier, n_dev - 1)
    for p in range(2):
        push_copy(p).start()

    below = lax.broadcasted_iota(jnp.int32, tri.shape, 0)
    across = lax.broadcasted_iota(jnp.int32, tri.shape, 1)
    tri[...] = jnp.where((across >= GROUP) | (below <= across), 1.0, 0.0).astype(tri.dtype)

    for copy in small:
        copy.wait()
    row_id = lax.broadcasted_iota(jnp.int32, (rows, LANES), 0)
    lane_id = lax.broadcasted_iota(jnp.int32, (rows, LANES), 1)
    tau = jnp.zeros((rows, LANES), jnp.float32)
    tgt = jnp.zeros((rows, LANES), jnp.int32)
    for b in range(rows):
        tau = jnp.where(row_id == b, tau_sm[b], tau)
        tgt = jnp.where(row_id == b, tgt_sm[b], tgt)
    reach = tgt - me * width - lane_id

    def blocks_of(x):
        return [x[:, j * LANES:(j + 1) * LANES] for j in range(x.shape[1] // LANES)]

    def softmax_step(col, z, top, total, pick):
        z = [zj * tau for zj in blocks_of(z)]
        peak = functools.reduce(jnp.maximum, z)
        new_top = jnp.maximum(top, jnp.max(peak, axis=1, keepdims=True))
        alpha = jnp.exp(top - new_top)
        e = [jnp.exp(zj - new_top) for zj in z]
        total = total * alpha + functools.reduce(jnp.add, e)
        hit = reach - col
        pick = pick * alpha + functools.reduce(
            jnp.add, [jnp.where(hit >= j * LANES, ej, 0.0) for j, ej in enumerate(e)]
        )
        return e, alpha, new_top, total, pick

    def prefix_step(col, e, base):
        groups = len(e) * LANES // GROUP
        stacked = jnp.concatenate([jnp.concatenate(e[2 * g:2 * g + 2], axis=1) for g in range(groups)], axis=0)
        sums = split_sums(stacked, tri)
        for g in range(groups):
            part_sums = sums[g * rows:(g + 1) * rows]
            for half in range(2):
                c_ref[:, pl.ds(col + (2 * g + half) * LANES, LANES)] = (
                    part_sums[:, half * LANES:(half + 1) * LANES] + base
                )
            base = base + part_sums[:, GROUP:]
        return base

    far[0] = jnp.full((rows, LANES), -jnp.inf, jnp.float32)
    for i in range(1, 4):
        far[i] = jnp.zeros((rows, LANES), jnp.float32)

    def far_step(p):
        z_copy(p).wait_recv()
        e, alpha, top, total, pick = softmax_step(far_col(p), z_in[p], far[0], far[2], far[3])
        far[1] = prefix_step(far_col(p), e, far[1] * alpha)
        far[0], far[2], far[3] = top, total, pick
        far_max[p] = top

    def full_step(t, state):
        top, base, total, pick = state
        slot, odd, p = lax.rem(t, RING), lax.rem(t, 2), lax.div(t, 2)

        @pl.when(odd == 1)
        def _():
            push_copy(p).wait_recv()
            z_out[p] = jnp.dot(h_buf[...], push_buf[p % SLOTS], preferred_element_type=jnp.float32)

        w_copy(0, slot).wait()
        z = jnp.dot(h_buf[...], w_buf[slot], preferred_element_type=jnp.float32)

        @pl.when(t + RING < n_full)
        def _():
            w_copy(t + RING, slot).start()

        @pl.when(t + RING == n_full)
        def _():
            for k in range(CHUNKS):
                last_copy(k).start()

        @pl.when(odd == 1)
        def _():
            z_copy(p).start()

        @pl.when((odd == 1) & (p + 2 < PUSHES))
        def _():
            push_copy(p + 2).start()

        e, alpha, top, total, pick = softmax_step(near_col(t), z, top, total, pick)
        base = prefix_step(near_col(t), e, base * alpha)
        near_max[t] = top

        @pl.when((odd == 0) & (t >= 4))
        def _():
            far_step(p - 2)

        return top, base, total, pick

    zero = jnp.zeros((rows, LANES), jnp.float32)
    start = (jnp.full((rows, LANES), -jnp.inf, jnp.float32), zero, zero, zero)
    top, base, total, pick = lax.fori_loop(0, n_full, full_step, start)

    far_step(PUSHES - 2)
    far_step(PUSHES - 1)
    z = jnp.zeros((rows, TILE), jnp.float32)
    for k in range(CHUNKS):
        last_copy(k).wait()
        rows_k = pl.ds(k * part, part)
        z = z + jnp.dot(h_buf[:, rows_k], w_buf[n_full % RING, rows_k, :], preferred_element_type=jnp.float32)
    e, alpha, near_top, total, pick = softmax_step(near_col(n_full), z, top, total, pick)

    top = jnp.maximum(near_top, far[0])
    near_scale, far_scale = jnp.exp(near_top - top), jnp.exp(far[0] - top)
    diag = row_id == lane_id
    to_lanes = lambda x: jnp.sum(jnp.where(diag, x, 0.0), axis=0, keepdims=True)
    row_sum = lambda x: jnp.broadcast_to(jnp.sum(x, axis=1, keepdims=True), x.shape)
    top_l = to_lanes(top)
    total_l = to_lanes(row_sum(total * near_scale + far[2] * far_scale))
    pick_l = to_lanes(row_sum(pick * near_scale + far[3] * far_scale))
    sub = lax.broadcasted_iota(jnp.int32, (8, LANES), 0)
    packet = jnp.where(sub == 0, top_l, jnp.where(sub == 1, total_l, jnp.where(sub == 2, pick_l, 0.0)))
    pack[...] = packet
    comm[me] = packet

    copies = [
        pltpu.make_async_remote_copy(
            src_ref=pack, dst_ref=comm.at[me], send_sem=send_sem.at[d - 1], recv_sem=recv_sem.at[d - 1],
            device_id=peer_id(d), device_id_type=MESH,
        )
        for d in range(1, n_dev)
    ]
    for copy in copies:
        copy.start()

    prefix_step(near_col(n_full), e, base * alpha)
    near_max[n_full] = near_top
    far_sum = far[1] * far_scale

    def rescale_near(t, carry):
        factor = jnp.exp(near_max[t] - top)
        for j in range(TILE // LANES):
            cols = pl.ds(near_col(t) + j * LANES, LANES)
            c_ref[:, cols] = c_ref[:, cols] * factor + far_sum
        return carry

    def rescale_far(p, carry):
        factor = jnp.exp(far_max[p] - top)
        for j in range(PUSH // LANES):
            cols = pl.ds(far_col(p) + j * LANES, LANES)
            c_ref[:, cols] = c_ref[:, cols] * factor
        return carry

    lax.fori_loop(0, n_full + 1, rescale_near, 0)
    lax.fori_loop(0, PUSHES, rescale_far, 0)
    for p in range(PUSHES):
        push_copy(p).wait_send()
        z_copy(p).wait_send()

    for copy in copies:
        copy.wait()
    tops, sums, picks = comm[:, 0, :], comm[:, 1, :], comm[:, 2, :]
    top_all = jnp.max(tops, axis=0, keepdims=True)
    scale = jnp.exp(tops - top_all)
    mass = sums * scale
    dev = lax.broadcasted_iota(jnp.int32, (n_dev, LANES), 0)
    all_mass = jnp.sum(mass, axis=0, keepdims=True)
    lower = jnp.sum(jnp.where(dev < me, mass, 0.0), axis=0, keepdims=True)
    picked = jnp.sum(picks * scale, axis=0, keepdims=True)
    mult = jnp.exp(top_l - top_all) / all_mass
    fin_ref[...] = jnp.where(
        sub == 0, mult, jnp.where(sub == 1, lower / all_mass, jnp.where(sub == 2, picked / all_mass, 0.0))
    )


def finish_kernel(c_ref, fin_ref, cdf_hbm, picked_hbm, out_buf, picked_buf, out_sem):
    rows, width = c_ref.shape
    step = width // OUT_CHUNKS
    row_id = lax.broadcasted_iota(jnp.int32, (rows, LANES), 0)
    lane_id = lax.broadcasted_iota(jnp.int32, (rows, LANES), 1)
    fin = fin_ref[...]
    to_rows = lambda x: jnp.broadcast_to(
        jnp.sum(jnp.where(row_id == lane_id, x, 0.0), axis=1, keepdims=True), (rows, LANES)
    )
    mult, offset = to_rows(fin[0:1]), to_rows(fin[1:2])
    picked_buf[...] = fin[2, :rows]
    copies = [pltpu.make_async_copy(picked_buf, picked_hbm, out_sem.at[OUT_CHUNKS])]
    copies[0].start()
    for i in range(OUT_CHUNKS):
        for j in range(step // LANES):
            cols = pl.ds(i * step + j * LANES, LANES)
            out_buf[:, cols] = c_ref[:, cols] * mult + offset
        cols = pl.ds(i * step, step)
        copies.append(pltpu.make_async_copy(out_buf.at[:, cols], cdf_hbm.at[:, cols], out_sem.at[i]))
        copies[-1].start()
    for copy in copies:
        copy.wait()


def solution(mesh):
    vblk_size, vocab_size = mesh.shape["vblk"], mesh.shape["vocab"]
    n_dev = vblk_size * vocab_size

    def local_step(hidden, w_head, inv_temp, target):
        rows, depth = hidden.shape
        width = w_head.shape[1]
        hbm = pl.BlockSpec(memory_space=pltpu.HBM)
        vmem = pl.BlockSpec(memory_space=pltpu.VMEM)
        mass, fin = pl.pallas_call(
            functools.partial(stream_kernel, vblk_size, vocab_size),
            out_shape=(
                jax.ShapeDtypeStruct((rows, width), jnp.float32),
                jax.ShapeDtypeStruct((8, LANES), jnp.float32),
            ),
            in_specs=[hbm] * 4,
            out_specs=(vmem, vmem),
            scratch_shapes=[
                pltpu.VMEM((rows, depth), jnp.bfloat16),
                pltpu.VMEM((RING, depth, TILE), jnp.bfloat16),
                pltpu.VMEM((SLOTS, depth, PUSH), jnp.bfloat16),
                pltpu.VMEM((PUSHES, rows, PUSH), jnp.float32),
                pltpu.VMEM((PUSHES, rows, PUSH), jnp.float32),
                pltpu.VMEM((GROUP, GROUP + LANES), jnp.bfloat16),
                pltpu.VMEM(((width - PUSH * PUSHES) // TILE, rows, LANES), jnp.float32),
                pltpu.VMEM((PUSHES, rows, LANES), jnp.float32),
                pltpu.VMEM((4, rows, LANES), jnp.float32),
                pltpu.VMEM((8, LANES), jnp.float32),
                pltpu.VMEM((n_dev, 8, LANES), jnp.float32),
                pltpu.SMEM((rows,), jnp.float32),
                pltpu.SMEM((rows,), jnp.int32),
                pltpu.SemaphoreType.DMA((3,)),
                pltpu.SemaphoreType.DMA((RING,)),
                pltpu.SemaphoreType.DMA((CHUNKS,)),
                pltpu.SemaphoreType.DMA((PUSHES,)),
                pltpu.SemaphoreType.DMA((PUSHES,)),
                pltpu.SemaphoreType.DMA((PUSHES,)),
                pltpu.SemaphoreType.DMA((PUSHES,)),
                pltpu.SemaphoreType.DMA((n_dev - 1,)),
                pltpu.SemaphoreType.DMA((n_dev - 1,)),
            ],
            compiler_params=pltpu.CompilerParams(
                collective_id=0, has_side_effects=True, vmem_limit_bytes=44 * 1024 * 1024
            ),
        )(*[pltpu.with_memory_space_constraint(x, pltpu.HBM) for x in (inv_temp, target, hidden, w_head)])
        return pl.pallas_call(
            finish_kernel,
            out_shape=(
                jax.ShapeDtypeStruct((rows, width), jnp.float32),
                jax.ShapeDtypeStruct((rows,), jnp.float32),
            ),
            in_specs=[vmem, vmem],
            out_specs=(hbm, hbm),
            scratch_shapes=[
                pltpu.VMEM((rows, width), jnp.float32),
                pltpu.VMEM((rows,), jnp.float32),
                pltpu.SemaphoreType.DMA((OUT_CHUNKS + 1,)),
            ],
            compiler_params=pltpu.CompilerParams(vmem_limit_bytes=8 * 1024 * 1024),
        )(mass, fin)

    vocab_axes = ("vblk", "vocab")
    return jax.shard_map(
        local_step,
        mesh=mesh,
        in_specs=(P("dp", None), P(None, vocab_axes), P("dp"), P("dp")),
        out_specs=(P("dp", vocab_axes), P("dp")),
        check_vma=False,
    )
```

time: 68.2 us -> 60 us (0.88)
  Pallas kernels: 65.4 us -> 59.2 us
  other arithmetic: 1.53 us -> 0 us
    pallas_call x1, Pallas kernels: 65.4 us -> 57.8 us  [local_step(): pl.pallas_call(functools.partial(stream_kernel, vblk_size, vocab_size), o...]
    add x1 -> x0, other arithmetic: 1.53 us -> none  [local_step(): cdf = mass * fin[0, :rows, None] + fin[1, :rows, None]]
    pallas_call x0 -> x1, Pallas kernels: none -> 1.46 us  [local_step(): pl.pallas_call(finish_kernel, out_shape=(jax.ShapeDtypeStruct((rows, widt...]
where the time goes in v2:
time: 60 us; the launch traced here: 59.9 us
  Pallas kernels  59.2 us (99%)
  between operations  0.64 us (1%)
    pallas_call x1, Pallas kernels, local_step(): pl.pallas_call(functools.partial(stream_kernel, vblk_size, vocab_size), o...  57.8 us
    pallas_call x1, Pallas kernels, local_step(): pl.pallas_call(finish_kernel, out_shape=(jax.ShapeDtypeStruct((rows, widt...  1.46 us

profile of v2, /device:TPU:0, one launch (start us, length us, event | category | flops | bytes accessed | tf_op | source)
XLA Modules:
  0.0 59.9 jit_solution(2370264503392687898)
XLA Ops:
  0.6 57.8 %shard_map.59 = (f32[16,32000]{1,0:T(8,128)S(1)}, f32[8,128]{1,0:T(8,128)S(1)}) custom-call(f32[16]{0:T(128)} %tau_hbm.1, s32[16]{0:T(128)} %tgt_hbm.1, bf16[16,3072]{1,0:T(8,128)(2,1)} %h_hbm.1, bf16[3072,32000]{1,0:T(8,128)(2,1)} %w_hbm.1), custom_call_target="tpu_custom_call" | custom-call | tf_op jit(solution)/shard_map/pallas_call | solution.py:301
  58.4 1.5 %shard_map.60 = (f32[16,32000]{1,0:T(8,128)}, f32[16]{0:T(128)}) custom-call(f32[16,32000]{1,0:T(8,128)S(1)} %get-tuple-element.4.c_ref, f32[8,128]{1,0:T(8,128)S(1)} %get-tuple-element.5.fin_ref), custom_call_target="tpu_custom_call" | custom-call | tf_op jit(solution)/shard_map/pallas_call | solution.py:337

commit v3 on v2

--- a/solution.py
+++ b/solution.py
@@ -10,9 +10,10 @@
 MESH = pl.DeviceIdType.MESH
 LANES = 128
 GROUP = 256
-TILE = 1280
-CHUNKS = 6
-RING = 3
+TILE = 1024
+LAST = 1280
+CHUNKS = (1536, 768, 512, 256)
+RING = 4
 PUSH = 512
 PUSHES = 10
 SLOTS = 4
@@ -31,15 +32,16 @@
 
 def stream_kernel(
     vblk_size, vocab_size, tau_hbm, tgt_hbm, h_hbm, w_hbm, c_ref, fin_ref,
-    h_buf, w_buf, push_buf, z_out, z_in, tri, near_max, far_max, far, pack, comm, tau_sm, tgt_sm,
-    in_sem, w_sem, last_sem, push_send, push_recv, z_send, z_recv, send_sem, recv_sem,
+    h_buf, w_buf, last_buf, push_buf, z_out, z_in, z_late, z_last, tri, near_max, far_max, far, pack, comm, tau_sm, tgt_sm,
+    ready, in_sem, w_sem, last_sem, push_send, push_recv, z_send, z_recv, send_sem, recv_sem,
 ):
     n_dev = vblk_size * vocab_size
     rows, depth = h_buf.shape
     width = w_hbm.shape[1]
     pushed = PUSH * PUSHES
-    n_full = (width - pushed) // TILE - 1
-    part = depth // CHUNKS
+    n_full = (width - pushed - LAST) // TILE
+    last_col = width - LAST
+    parts = [pl.ds(sum(CHUNKS[:k]), size) for k, size in enumerate(CHUNKS)]
     vblk, vocab = lax.axis_index("vblk"), lax.axis_index("vocab")
     me = vblk * vocab_size + vocab
     chip, core = lax.div(vocab, 2), lax.rem(vocab, 2)
@@ -60,9 +62,7 @@
 
     def last_copy(k):
         return pltpu.make_async_copy(
-            w_hbm.at[pl.ds(k * part, part), pl.ds(near_col(n_full), TILE)],
-            w_buf.at[n_full % RING, pl.ds(k * part, part)],
-            last_sem.at[k],
+            w_hbm.at[parts[k], pl.ds(last_col, LAST)], last_buf.at[parts[k]], last_sem.at[k]
         )
 
     def push_copy(p):
@@ -78,8 +78,10 @@
         )
 
     barrier = pltpu.get_barrier_semaphore()
-    for d in range(1, n_dev):
-        pl.semaphore_signal(barrier, inc=1, device_id=peer_id(d), device_id_type=MESH)
+
+    @pl.when(core == 0)
+    def _():
+        pl.semaphore_signal(barrier, inc=1, device_id=sibling, device_id_type=MESH)
 
     small = [
         pltpu.make_async_copy(h_hbm, h_buf, in_sem.at[0]),
@@ -91,7 +93,17 @@
     for t in range(RING):
         w_copy(t, t).start()
 
-    pl.semaphore_wait(barrier, n_dev - 1)
+    @pl.when(core == 1)
+    def _():
+        pl.semaphore_wait(barrier, 1)
+        pl.semaphore_signal(ready, inc=1, device_id=sibling, device_id_type=MESH)
+
+    @pl.when(core == 0)
+    def _():
+        pl.semaphore_wait(ready, 1)
+        for d in range(2, n_dev, 2):
+            pl.semaphore_signal(barrier, inc=1, device_id=peer_id(d), device_id_type=MESH)
+
     for p in range(2):
         push_copy(p).start()
 
@@ -150,57 +162,90 @@
         far[0], far[2], far[3] = top, total, pick
         far_max[p] = top
 
-    def full_step(t, state):
+    def near_step(t, z, state):
         top, base, total, pick = state
-        slot, odd, p = lax.rem(t, RING), lax.rem(t, 2), lax.div(t, 2)
-
-        @pl.when(odd == 1)
-        def _():
-            push_copy(p).wait_recv()
-            z_out[p] = jnp.dot(h_buf[...], push_buf[p % SLOTS], preferred_element_type=jnp.float32)
-
-        w_copy(0, slot).wait()
-        z = jnp.dot(h_buf[...], w_buf[slot], preferred_element_type=jnp.float32)
-
-        @pl.when(t + RING < n_full)
-        def _():
-            w_copy(t + RING, slot).start()
-
-        @pl.when(t + RING == n_full)
-        def _():
-            for k in range(CHUNKS):
-                last_copy(k).start()
-
-        @pl.when(odd == 1)
-        def _():
-            z_copy(p).start()
-
-        @pl.when((odd == 1) & (p + 2 < PUSHES))
-        def _():
-            push_copy(p + 2).start()
-
         e, alpha, top, total, pick = softmax_step(near_col(t), z, top, total, pick)
         base = prefix_step(near_col(t), e, base * alpha)
         near_max[t] = top
-
-        @pl.when((odd == 0) & (t >= 4))
+        return top, base, total, pick
+
+    def near_dot(t):
+        slot = lax.rem(t, RING)
+        w_copy(0, slot).wait()
+        return jnp.dot(h_buf[...], w_buf[slot], preferred_element_type=jnp.float32)
+
+    def refill(t):
+        @pl.when(t + RING < n_full)
         def _():
+            w_copy(t + RING, lax.rem(t, RING)).start()
+
+        @pl.when(t + RING == n_full)
+        def _():
+            for k in range(len(CHUNKS)):
+                last_copy(k).start()
+
+    def push_dot(p):
+        push_copy(p).wait_recv()
+        z_out[p] = jnp.dot(h_buf[...], push_buf[lax.rem(p, SLOTS)], preferred_element_type=jnp.float32)
+
+    def answer(p):
+        z_copy(p).start()
+
+        @pl.when(p + 2 < PUSHES)
+        def _():
+            push_copy(p + 2).start()
+
+    def round_step(u, state, first=False):
+        t, p = 5 * u, 2 * u
+        z = near_dot(t)
+        if not first:
+            state = near_step(t - 1, z_late[...], state)
             far_step(p - 2)
-
-        return top, base, total, pick
+        refill(t)
+        z_next = near_dot(t + 1)
+        state = near_step(t, z, state)
+        refill(t + 1)
+        z = near_dot(t + 2)
+        state = near_step(t + 1, z_next, state)
+        refill(t + 2)
+        push_dot(p)
+        z_next = near_dot(t + 3)
+        state = near_step(t + 2, z, state)
+        answer(p)
+        if not first:
+            far_step(p - 1)
+        refill(t + 3)
+        z = near_dot(t + 4)
+        z_late[...] = z
+        refill(t + 4)
+        push_dot(p + 1)
+        state = near_step(t + 3, z_next, state)
+        answer(p + 1)
+        return state
 
     zero = jnp.zeros((rows, LANES), jnp.float32)
-    start = (jnp.full((rows, LANES), -jnp.inf, jnp.float32), zero, zero, zero)
-    top, base, total, pick = lax.fori_loop(0, n_full, full_step, start)
-
+    state = (jnp.full((rows, LANES), -jnp.inf, jnp.float32), zero, zero, zero)
+    state = round_step(jnp.int32(0), state, first=True)
+    state = lax.fori_loop(1, n_full // 5, round_step, state)
+
+    @pl.when(core == 0)
+    def _():
+        pl.semaphore_wait(barrier, n_dev // 2 - 1)
+        pl.semaphore_signal(ready, inc=1, device_id=sibling, device_id_type=MESH)
+
+    def last_dot(k):
+        last_copy(k).wait()
+        return jnp.dot(h_buf[:, parts[k]], last_buf[parts[k], :], preferred_element_type=jnp.float32)
+
+    z_last[...] = last_dot(0)
+    top, base, total, pick = near_step(n_full - 1, z_late[...], state)
     far_step(PUSHES - 2)
+    z_last[...] += last_dot(1)
     far_step(PUSHES - 1)
-    z = jnp.zeros((rows, TILE), jnp.float32)
-    for k in range(CHUNKS):
-        last_copy(k).wait()
-        rows_k = pl.ds(k * part, part)
-        z = z + jnp.dot(h_buf[:, rows_k], w_buf[n_full % RING, rows_k, :], preferred_element_type=jnp.float32)
-    e, alpha, near_top, total, pick = softmax_step(near_col(n_full), z, top, total, pick)
+    z = z_last[...]
+    for k in range(2, len(CHUNKS)):
+        z = z + last_dot(k)
+    e, alpha, near_top, total, pick = softmax_step(last_col, z, top, total, pick)
 
     top = jnp.maximum(near_top, far[0])
     near_scale, far_scale = jnp.exp(near_top - top), jnp.exp(far[0] - top)
@@ -215,6 +260,10 @@
     pack[...] = packet
     comm[me] = packet
 
+    @pl.when(core == 1)
+    def _():
+        pl.semaphore_wait(ready, 1)
+
     copies = [
         pltpu.make_async_remote_copy(
             src_ref=pack, dst_ref=comm.at[me], send_sem=send_sem.at[d - 1], recv_sem=recv_sem.at[d - 1],
@@ -225,8 +274,7 @@
     for copy in copies:
         copy.start()
 
-    prefix_step(near_col(n_full), e, base * alpha)
-    near_max[n_full] = near_top
+    prefix_step(last_col, e, base * alpha)
     far_sum = far[1] * far_scale
 
     def rescale_near(t, carry):
@@ -243,7 +291,10 @@
             c_ref[:, cols] = c_ref[:, cols] * factor
         return carry
 
-    lax.fori_loop(0, n_full + 1, rescale_near, 0)
+    lax.fori_loop(0, n_full, rescale_near, 0)
+    for j in range(LAST // LANES):
+        cols = pl.ds(last_col + j * LANES, LANES)
+        c_ref[:, cols] = c_ref[:, cols] * near_scale + far_sum
     lax.fori_loop(0, PUSHES, rescale_far, 0)
     for p in range(PUSHES):
         push_copy(p).wait_send()
@@ -309,20 +360,24 @@
             scratch_shapes=[
                 pltpu.VMEM((rows, depth), jnp.bfloat16),
                 pltpu.VMEM((RING, depth, TILE), jnp.bfloat16),
+                pltpu.VMEM((depth, LAST), jnp.bfloat16),
                 pltpu.VMEM((SLOTS, depth, PUSH), jnp.bfloat16),
                 pltpu.VMEM((PUSHES, rows, PUSH), jnp.float32),
                 pltpu.VMEM((PUSHES, rows, PUSH), jnp.float32),
+                pltpu.VMEM((rows, TILE), jnp.float32),
+                pltpu.VMEM((rows, LAST), jnp.float32),
                 pltpu.VMEM((GROUP, GROUP + LANES), jnp.bfloat16),
-                pltpu.VMEM(((width - PUSH * PUSHES) // TILE, rows, LANES), jnp.float32),
+                pltpu.VMEM(((width - PUSH * PUSHES - LAST) // TILE, rows, LANES), jnp.float32),
                 pltpu.VMEM((PUSHES, rows, LANES), jnp.float32),
                 pltpu.VMEM((4, rows, LANES), jnp.float32),
                 pltpu.VMEM((8, LANES), jnp.float32),
                 pltpu.VMEM((n_dev, 8, LANES), jnp.float32),
                 pltpu.SMEM((rows,), jnp.float32),
                 pltpu.SMEM((rows,), jnp.int32),
+                pltpu.SemaphoreType.REGULAR,
                 pltpu.SemaphoreType.DMA((3,)),
                 pltpu.SemaphoreType.DMA((RING,)),
-                pltpu.SemaphoreType.DMA((CHUNKS,)),
+                pltpu.SemaphoreType.DMA((len(CHUNKS),)),
                 pltpu.SemaphoreType.DMA((PUSHES,)),
                 pltpu.SemaphoreType.DMA((PUSHES,)),
                 pltpu.SemaphoreType.DMA((PUSHES,)),
@@ -331,7 +386,7 @@
                 pltpu.SemaphoreType.DMA((n_dev - 1,)),
             ],
             compiler_params=pltpu.CompilerParams(
-                collective_id=0, has_side_effects=True, vmem_limit_bytes=44 * 1024 * 1024
+                collective_id=0, has_side_effects=True, vmem_limit_bytes=48 * 1024 * 1024
             ),
         )(*[pltpu.with_memory_space_constraint(x, pltpu.HBM) for x in (inv_temp, target, hidden, w_head)])
         return pl.pallas_call(

time: 60 us -> 58.8 us (0.980)
  Pallas kernels: 59.2 us -> 58.1 us
    pallas_call x1, Pallas kernels: 57.8 us -> 56.7 us  [local_step(): pl.pallas_call(functools.partial(stream_kernel, vblk_size, vocab_size), o...]
where the time goes in v3:
time: 58.8 us
  Pallas kernels  58.1 us (99%)
  between operations  0.64 us (1%)
    pallas_call x1, Pallas kernels, local_step(): pl.pallas_call(functools.partial(stream_kernel, vblk_size, vocab_size), o...  56.7 us
    pallas_call x1, Pallas kernels, local_step(): pl.pallas_call(finish_kernel, out_shape=(jax.ShapeDtypeStruct((rows, widt...  1.46 us

profile of v3, /device:TPU:0, one launch (start us, length us, event | category | flops | bytes accessed | tf_op | source)
XLA Modules:
  0.0 58.8 jit_solution(3860792860293700486)
XLA Ops:
  0.6 56.7 %shard_map.59 = (f32[16,32000]{1,0:T(8,128)S(1)}, f32[8,128]{1,0:T(8,128)S(1)}) custom-call(f32[16]{0:T(128)} %tau_hbm.1, s32[16]{0:T(128)} %tgt_hbm.1, bf16[16,3072]{1,0:T(8,128)(2,1)} %h_hbm.1, bf16[3072,32000]{1,0:T(8,128)(2,1)} %w_hbm.1), custom_call_target="tpu_custom_call" | custom-call | tf_op jit(solution)/shard_map/pallas_call | solution.py:352
  57.3 1.5 %shard_map.60 = (f32[16,32000]{1,0:T(8,128)}, f32[16]{0:T(128)}) custom-call(f32[16,32000]{1,0:T(8,128)S(1)} %get-tuple-element.4.c_ref, f32[8,128]{1,0:T(8,128)S(1)} %get-tuple-element.5.fin_ref), custom_call_target="tpu_custom_call" | custom-call | tf_op jit(solution)/shard_map/pallas_call | solution.py:392

commit v4 on v3

--- a/solution.py
+++ b/solution.py
@@ -32,7 +32,7 @@
 
 def stream_kernel(
     vblk_size, vocab_size, tau_hbm, tgt_hbm, h_hbm, w_hbm, c_ref, fin_ref,
-    h_buf, w_buf, last_buf, push_buf, z_out, z_in, z_late, z_last, tri, near_max, far_max, far, pack, comm, tau_sm, tgt_sm,
+    h_buf, w_buf, last_buf, push_buf, z_out, z_in, z_late, z_last, tri, near_max, far_max, far, guest, pack, comm, tau_sm, tgt_sm,
     ready, in_sem, w_sem, last_sem, push_send, push_recv, z_send, z_recv, send_sem, recv_sem,
 ):
     n_dev = vblk_size * vocab_size
@@ -121,11 +121,13 @@
         tau = jnp.where(row_id == b, tau_sm[b], tau)
         tgt = jnp.where(row_id == b, tgt_sm[b], tgt)
     reach = tgt - me * width - lane_id
+    host = vblk * vocab_size + chip * 2 + (1 - core)
+    guest_reach = tgt - host * width - lane_id
 
     def blocks_of(x):
         return [x[:, j * LANES:(j + 1) * LANES] for j in range(x.shape[1] // LANES)]
 
-    def softmax_step(col, z, top, total, pick):
+    def softmax_step(col, z, top, total, pick, reach=reach):
         z = [zj * tau for zj in blocks_of(z)]
         peak = functools.reduce(jnp.maximum, z)
         new_top = jnp.maximum(top, jnp.max(peak, axis=1, keepdims=True))
@@ -151,15 +153,15 @@
             base = base + part_sums[:, GROUP:]
         return base
 
-    far[0] = jnp.full((rows, LANES), -jnp.inf, jnp.float32)
-    for i in range(1, 4):
-        far[i] = jnp.zeros((rows, LANES), jnp.float32)
+    lowest, zero = jnp.full((rows, LANES), -jnp.inf, jnp.float32), jnp.zeros((rows, LANES), jnp.float32)
+    far[0], far[1] = lowest, zero
+    guest[0], guest[1], guest[2] = lowest, zero, zero
 
     def far_step(p):
         z_copy(p).wait_recv()
-        e, alpha, top, total, pick = softmax_step(far_col(p), z_in[p], far[0], far[2], far[3])
+        e, alpha, top, _, _ = softmax_step(far_col(p), z_in[p], far[0], zero, zero)
         far[1] = prefix_step(far_col(p), e, far[1] * alpha)
-        far[0], far[2], far[3] = top, total, pick
+        far[0] = top
         far_max[p] = top
 
     def near_step(t, z, state):
@@ -186,7 +188,9 @@
 
     def push_dot(p):
         push_copy(p).wait_recv()
-        z_out[p] = jnp.dot(h_buf[...], push_buf[lax.rem(p, SLOTS)], preferred_element_type=jnp.float32)
+        z = jnp.dot(h_buf[...], push_buf[lax.rem(p, SLOTS)], preferred_element_type=jnp.float32)
+        z_out[p] = z
+        _, _, guest[0], guest[1], guest[2] = softmax_step(far_col(p), z, guest[0], guest[1], guest[2], guest_reach)
 
     def answer(p):
         z_copy(p).start()
@@ -223,8 +227,7 @@
         answer(p + 1)
         return state
 
-    zero = jnp.zeros((rows, LANES), jnp.float32)
-    state = (jnp.full((rows, LANES), -jnp.inf, jnp.float32), zero, zero, zero)
+    state = (lowest, zero, zero, zero)
     state = round_step(jnp.int32(0), state, first=True)
     state = lax.fori_loop(1, n_full // 5, round_step, state)
 
@@ -239,24 +242,20 @@
 
     z_last[...] = last_dot(0)
     top, base, total, pick = near_step(n_full - 1, z_late[...], state)
-    far_step(PUSHES - 2)
     z_last[...] += last_dot(1)
-    far_step(PUSHES - 1)
     z = z_last[...]
     for k in range(2, len(CHUNKS)):
         z = z + last_dot(k)
     e, alpha, near_top, total, pick = softmax_step(last_col, z, top, total, pick)
 
-    top = jnp.maximum(near_top, far[0])
-    near_scale, far_scale = jnp.exp(near_top - top), jnp.exp(far[0] - top)
     diag = row_id == lane_id
     to_lanes = lambda x: jnp.sum(jnp.where(diag, x, 0.0), axis=0, keepdims=True)
     row_sum = lambda x: jnp.broadcast_to(jnp.sum(x, axis=1, keepdims=True), x.shape)
-    top_l = to_lanes(top)
-    total_l = to_lanes(row_sum(total * near_scale + far[2] * far_scale))
-    pick_l = to_lanes(row_sum(pick * near_scale + far[3] * far_scale))
     sub = lax.broadcasted_iota(jnp.int32, (8, LANES), 0)
-    packet = jnp.where(sub == 0, top_l, jnp.where(sub == 1, total_l, jnp.where(sub == 2, pick_l, 0.0)))
+    packet = jnp.zeros((8, LANES), jnp.float32)
+    stats = (near_top, row_sum(total), row_sum(pick), guest[0], row_sum(guest[1]), row_sum(guest[2]))
+    for i, stat in enumerate(stats):
+        packet = jnp.where(sub == i, to_lanes(stat), packet)
     pack[...] = packet
     comm[me] = packet
 
@@ -274,6 +273,10 @@
     for copy in copies:
         copy.start()
 
+    far_step(PUSHES - 2)
+    far_step(PUSHES - 1)
+    top = jnp.maximum(near_top, far[0])
+    near_scale, far_scale = jnp.exp(near_top - top), jnp.exp(far[0] - top)
     prefix_step(last_col, e, base * alpha)
     far_sum = far[1] * far_scale
 
@@ -302,15 +305,16 @@
 
     for copy in copies:
         copy.wait()
-    tops, sums, picks = comm[:, 0, :], comm[:, 1, :], comm[:, 2, :]
-    top_all = jnp.max(tops, axis=0, keepdims=True)
-    scale = jnp.exp(tops - top_all)
-    mass = sums * scale
     dev = lax.broadcasted_iota(jnp.int32, (n_dev, LANES), 0)
-    all_mass = jnp.sum(mass, axis=0, keepdims=True)
-    lower = jnp.sum(jnp.where(dev < me, mass, 0.0), axis=0, keepdims=True)
-    picked = jnp.sum(picks * scale, axis=0, keepdims=True)
-    mult = jnp.exp(top_l - top_all) / all_mass
+    hosts = dev + 1 - 2 * lax.rem(dev, 2)
+    tops, guest_tops = comm[:, 0, :], comm[:, 3, :]
+    top_all = jnp.max(jnp.maximum(tops, guest_tops), axis=0, keepdims=True)
+    scale, guest_scale = jnp.exp(tops - top_all), jnp.exp(guest_tops - top_all)
+    mass, guest_mass = comm[:, 1, :] * scale, comm[:, 4, :] * guest_scale
+    all_mass = jnp.sum(mass + guest_mass, axis=0, keepdims=True)
+    lower = jnp.sum(jnp.where(dev < me, mass, 0.0) + jnp.where(hosts < me, guest_mass, 0.0), axis=0, keepdims=True)
+    picked = jnp.sum(comm[:, 2, :] * scale + comm[:, 5, :] * guest_scale, axis=0, keepdims=True)
+    mult = jnp.exp(to_lanes(top) - top_all) / all_mass
     fin_ref[...] = jnp.where(
         sub == 0, mult, jnp.where(sub == 1, lower / all_mass, jnp.where(sub == 2, picked / all_mass, 0.0))
     )
@@ -369,7 +373,8 @@
                 pltpu.VMEM((GROUP, GROUP + LANES), jnp.bfloat16),
                 pltpu.VMEM(((width - PUSH * PUSHES - LAST) // TILE, rows, LANES), jnp.float32),
                 pltpu.VMEM((PUSHES, rows, LANES), jnp.float32),
-                pltpu.VMEM((4, rows, LANES), jnp.float32),
+                pltpu.VMEM((2, rows, LANES), jnp.float32),
+                pltpu.VMEM((3, rows, LANES), jnp.float32),
                 pltpu.VMEM((8, LANES), jnp.float32),
                 pltpu.VMEM((n_dev, 8, LANES), jnp.float32),
                 pltpu.SMEM((rows,), jnp.float32),

time: 58.8 us -> 58.3 us (level)
  no operation moved by 1% of the time
where the time goes in v4:
time: 58.3 us; the launch traced here: 58.2 us
  Pallas kernels  57.6 us (99%)
  between operations  0.64 us (1%)
    pallas_call x1, Pallas kernels, local_step(): pl.pallas_call(functools.partial(stream_kernel, vblk_size, vocab_size), o...  56.2 us
    pallas_call x1, Pallas kernels, local_step(): pl.pallas_call(finish_kernel, out_shape=(jax.ShapeDtypeStruct((rows, widt...  1.46 us

profile of v4, /device:TPU:0, one launch (start us, length us, event | category | flops | bytes accessed | tf_op | source)
XLA Modules:
  0.0 58.2 jit_solution(4140094887625070834)
XLA Ops:
  0.6 56.2 %shard_map.59 = (f32[16,32000]{1,0:T(8,128)S(1)}, f32[8,128]{1,0:T(8,128)S(1)}) custom-call(f32[16]{0:T(128)} %tau_hbm.1, s32[16]{0:T(128)} %tgt_hbm.1, bf16[16,3072]{1,0:T(8,128)(2,1)} %h_hbm.1, bf16[3072,32000]{1,0:T(8,128)(2,1)} %w_hbm.1), custom_call_target="tpu_custom_call" | custom-call | tf_op jit(solution)/shard_map/pallas_call | solution.py:356
  56.8 1.5 %shard_map.60 = (f32[16,32000]{1,0:T(8,128)}, f32[16]{0:T(128)}) custom-call(f32[16,32000]{1,0:T(8,128)S(1)} %get-tuple-element.4.c_ref, f32[8,128]{1,0:T(8,128)S(1)} %get-tuple-element.5.fin_ref), custom_call_target="tpu_custom_call" | custom-call | tf_op jit(solution)/shard_map/pallas_call | solution.py:397

commit v5 on v4

--- a/solution.py
+++ b/solution.py
@@ -12,7 +12,7 @@
 GROUP = 256
 TILE = 1024
 LAST = 1280
-CHUNKS = (1536, 768, 512, 256)
+CHUNKS = (2048, 1024)
 RING = 4
 PUSH = 512
 PUSHES = 10
@@ -90,7 +90,7 @@
     ]
     for copy in small:
         copy.start()
-    for t in range(RING):
+    for t in range(RING - 1):
         w_copy(t, t).start()
 
     @pl.when(core == 1)
@@ -172,19 +172,19 @@
         return top, base, total, pick
 
     def near_dot(t):
-        slot = lax.rem(t, RING)
+        slot, ahead = lax.rem(t, RING), t + RING - 1
         w_copy(0, slot).wait()
-        return jnp.dot(h_buf[...], w_buf[slot], preferred_element_type=jnp.float32)
-
-    def refill(t):
-        @pl.when(t + RING < n_full)
+
+        @pl.when(ahead < n_full)
         def _():
-            w_copy(t + RING, lax.rem(t, RING)).start()
-
-        @pl.when(t + RING == n_full)
+            w_copy(ahead, lax.rem(ahead, RING)).start()
+
+        @pl.when(ahead == n_full)
         def _():
             for k in range(len(CHUNKS)):
                 last_copy(k).start()
+
+        return jnp.dot(h_buf[...], w_buf[slot], preferred_element_type=jnp.float32)
 
     def push_dot(p):
         push_copy(p).wait_recv()
@@ -205,23 +205,18 @@
         if not first:
             state = near_step(t - 1, z_late[...], state)
             far_step(p - 2)
-        refill(t)
         z_next = near_dot(t + 1)
         state = near_step(t, z, state)
-        refill(t + 1)
         z = near_dot(t + 2)
         state = near_step(t + 1, z_next, state)
-        refill(t + 2)
         push_dot(p)
         z_next = near_dot(t + 3)
         state = near_step(t + 2, z, state)
         answer(p)
         if not first:
             far_step(p - 1)
-        refill(t + 3)
         z = near_dot(t + 4)
         z_late[...] = z
-        refill(t + 4)
         push_dot(p + 1)
         state = near_step(t + 3, z_next, state)
         answer(p + 1)
@@ -242,9 +237,8 @@
 
     z_last[...] = last_dot(0)
     top, base, total, pick = near_step(n_full - 1, z_late[...], state)
-    z_last[...] += last_dot(1)
     z = z_last[...]
-    for k in range(2, len(CHUNKS)):
+    for k in range(1, len(CHUNKS)):
         z = z + last_dot(k)
     e, alpha, near_top, total, pick = softmax_step(last_col, z, top, total, pick)
 

time: 58.3 us -> 58.3 us (level)
  no operation moved by 1% of the time
where the time goes in v5:
time: 58.3 us; the launch traced here: 58.2 us
  Pallas kernels  57.5 us (99%)
  between operations  0.64 us (1%)
    pallas_call x1, Pallas kernels, local_step(): pl.pallas_call(functools.partial(stream_kernel, vblk_size, vocab_size), o...  56.1 us
    pallas_call x1, Pallas kernels, local_step(): pl.pallas_call(finish_kernel, out_shape=(jax.ShapeDtypeStruct((rows, widt...  1.46 us

profile of v5, /device:TPU:0, one launch (start us, length us, event | category | flops | bytes accessed | tf_op | source)
XLA Modules:
  0.0 58.2 jit_solution(6098357583439018924)
XLA Ops:
  0.6 56.1 %shard_map.59 = (f32[16,32000]{1,0:T(8,128)S(1)}, f32[8,128]{1,0:T(8,128)S(1)}) custom-call(f32[16]{0:T(128)} %tau_hbm.1, s32[16]{0:T(128)} %tgt_hbm.1, bf16[16,3072]{1,0:T(8,128)(2,1)} %h_hbm.1, bf16[3072,32000]{1,0:T(8,128)(2,1)} %w_hbm.1), custom_call_target="tpu_custom_call" | custom-call | tf_op jit(solution)/shard_map/pallas_call | solution.py:350
  56.7 1.5 %shard_map.60 = (f32[16,32000]{1,0:T(8,128)}, f32[16]{0:T(128)}) custom-call(f32[16,32000]{1,0:T(8,128)S(1)} %get-tuple-element.4.c_ref, f32[8,128]{1,0:T(8,128)S(1)} %get-tuple-element.5.fin_ref), custom_call_target="tpu_custom_call" | custom-call | tf_op jit(solution)/shard_map/pallas_call | solution.py:391
